TPU v7x, 32 devices: a 4x4x1 block of a 4x4x8 slice. The times are simulated.
32 devices in a mesh: batch: 1 (over z), tmpl: 4 (over y), dap: 8 (over x, core).
Axes of the slice: x: 4, y: 4, z: 1, core: 2. Of those that a mesh axis runs over, the one named last changes fastest.
The devices are a block of a 4x4x8 slice.
Arguments:
- tmpl_act: bfloat16 [4, 512, 512, 64], P(('batch', 'tmpl'), 'dap')
- tmpl_mask: int32 [4], P('batch')
- pair_act: bfloat16 [512, 512, 128], P(('batch', 'dap'))
- pair_mask: int32 [512, 512], P(('batch', 'dap'))
- ln_tri: float32 [2, 2, 64], replicated
- w_ab: bfloat16 [2, 64, 4, 64], replicated
- b_ab: float32 [2, 4, 64], replicated
- w_gate: bfloat16 [2, 64, 64], replicated
- b_gate: float32 [2, 64], replicated
- ln_mix: float32 [2, 2, 64], replicated
- w_mix: bfloat16 [2, 64, 64], replicated
- b_mix: float32 [2, 64], replicated
- ln_tr: float32 [2, 2, 64], replicated
- w_up: bfloat16 [2, 64, 128], replicated
- b_up: float32 [2, 128], replicated
- w_down: bfloat16 [2, 128, 64], replicated
- b_down: float32 [2, 64], replicated
- ln_fin: float32 [2, 64], replicated
- w_query: bfloat16 [128, 4, 16], replicated
- w_key: bfloat16 [64, 4, 16], replicated
- w_value: bfloat16 [64, 4, 16], replicated
- w_out: bfloat16 [4, 16, 128], replicated
- b_out: float32 [128], replicated
Outputs:
- output: bfloat16 [512, 512, 128], P(('batch', 'dap'))
All inputs are finite; a program needn't handle non-finite values.
Results may differ from a plain program's by a relative error of at most 0.0158191.
Values are sent between devices in bfloat16 or wider.
A program may use at most 768 MiB of HBM per device.

v0:
```python
import jax
import jax.numpy as jnp
from jax import lax
from jax.sharding import PartitionSpec as P

LN_EPS = 1e-5
MASK_BIAS = 1e9
BLOCK_ARGS = 13


def layer_norm(values, gain_bias):
    val_f32 = values.astype(jnp.float32)
    row_mean = jnp.mean(val_f32, axis=-1, keepdims=True)
    centered = val_f32 - row_mean
    row_var = jnp.mean(centered * centered, axis=-1, keepdims=True)
    scaled = centered * lax.rsqrt(row_var + LN_EPS)
    return (scaled * gain_bias[0] + gain_bias[1]).astype(jnp.bfloat16)


def pair_block(tmpl_loc, mask_f, block_w):
    ln_tri, w_ab, b_ab, w_gate, b_gate, ln_mix, w_mix, b_mix, ln_tr, w_up, b_up, w_down, b_down = block_w
    normed = layer_norm(tmpl_loc, ln_tri)
    proj_all = jnp.einsum('sikc,cgm->gsikm', normed, w_ab, preferred_element_type=jnp.float32)
    proj_all = proj_all + b_ab[:, None, None, None, :]
    left_act = (jax.nn.sigmoid(proj_all[0]) * proj_all[1] * mask_f).astype(jnp.bfloat16)
    right_act = (jax.nn.sigmoid(proj_all[2]) * proj_all[3] * mask_f).astype(jnp.bfloat16)
    right_all = lax.all_gather(right_act, 'dap', axis=1, tiled=True)
    mixed_sum = jnp.einsum('sikc,sjkc->sijc', left_act, right_all, preferred_element_type=jnp.float32)
    update = jnp.dot(layer_norm(mixed_sum, ln_mix), w_mix, preferred_element_type=jnp.float32) + b_mix
    gate_val = jax.nn.sigmoid(jnp.dot(normed, w_gate, preferred_element_type=jnp.float32) + b_gate)
    tmpl_loc = (tmpl_loc.astype(jnp.float32) + gate_val * update).astype(jnp.bfloat16)
    normed = layer_norm(tmpl_loc, ln_tr)
    hidden = jax.nn.relu(jnp.dot(normed, w_up, preferred_element_type=jnp.float32) + b_up).astype(jnp.bfloat16)
    update = jnp.dot(hidden, w_down, preferred_element_type=jnp.float32) + b_down
    return (tmpl_loc.astype(jnp.float32) + update).astype(jnp.bfloat16)


def pointwise_attend(tmpl_all, tmpl_mask, pair_loc, w_query, w_key, w_value, w_out, b_out):
    head_dim = w_query.shape[2]
    query_act = jnp.einsum('ijc,chd->ijhd', pair_loc, w_query, preferred_element_type=jnp.float32).astype(jnp.bfloat16)
    key_act = jnp.einsum('sijc,chd->sijhd', tmpl_all, w_key, preferred_element_type=jnp.float32).astype(jnp.bfloat16)
    value_act = jnp.einsum('sijc,chd->sijhd', tmpl_all, w_value, preferred_element_type=jnp.float32).astype(jnp.bfloat16)
    bias_tmpl = MASK_BIAS * (tmpl_mask.astype(jnp.float32) - 1.0)
    logits = jnp.einsum('ijhd,sijhd->ijhs', query_act, key_act, preferred_element_type=jnp.float32) * head_dim ** -0.5 + bias_tmpl
    prob_act = jax.nn.softmax(logits, axis=-1).astype(jnp.bfloat16)
    attended = jnp.einsum('ijhs,sijhd->ijhd', prob_act, value_act, preferred_element_type=jnp.float32).astype(jnp.bfloat16)
    update = jnp.einsum('ijhd,hdc->ijc', attended, w_out, preferred_element_type=jnp.float32) + b_out
    return (pair_loc.astype(jnp.float32) + update).astype(jnp.bfloat16)


def solution(mesh):
    tmpl_spec = P(('batch', 'tmpl'), 'dap')
    row_spec = P(('batch', 'dap'))

    def local_fn(tmpl_loc, tmpl_mask, pair_loc, mask_loc, *weights):
        mask_f = mask_loc.astype(jnp.float32)[None, :, :, None]
        block_stack = weights[:BLOCK_ARGS]
        ln_fin, w_query, w_key, w_value, w_out, b_out = weights[BLOCK_ARGS:]
        for block_idx in range(block_stack[0].shape[0]):
            tmpl_loc = pair_block(tmpl_loc, mask_f, tuple(stacked_w[block_idx] for stacked_w in block_stack))
        tmpl_fin = layer_norm(tmpl_loc, ln_fin)
        tmpl_all = lax.all_gather(tmpl_fin, 'tmpl', axis=0, tiled=True)
        return pointwise_attend(tmpl_all, tmpl_mask, pair_loc, w_query, w_key, w_value, w_out, b_out)

    in_specs = (tmpl_spec, P('batch'), row_spec, row_spec) + (P(),) * (BLOCK_ARGS + 6)
    return jax.shard_map(local_fn, mesh=mesh, in_specs=in_specs, out_specs=row_spec, check_vma=False)
```

profile of v0, /device:TPU:97, one launch (start us, length us, event | category | flops | bytes accessed | tf_op | source)
XLA Modules:
  0.0 739.5 jit_solution(10065769175849780121)
XLA Ops:
  9.2 3.5 convert_reduce_fusion.3
  12.7 3.9 fusion.40
  16.7 13.3 %fusion.1 = f32[4,1,64,512,64]{3,4,0,2,1:T(8,128)} fusion(f32[4,64]{1,0:T(4,128)S(1)} %get-tuple-element.8, bf16[1,64,4,64]{1,3,2,0:T(8,128)(2,1)S(1)} %copy.100, bf16[1,64,512,64]{2,3,1,0:T(8,128)(2,1)S(1)} %copy-done.1, f32[64]{0:T(128)S(1)} %get-tuple-element.18, f32[64]{0:T(128)S(1)} %get-tuple-element.19, f32[64,512]{1,0:T(8,128)S(1)} %add_rsqrt_fusion.6, ...), kind=kOutput, calls=%fused_computation.3 | convolution fusion | flops 1094713344 | bytes 38045184 | tf_op jit(solution)/shard_map/sikc,cgm->gsikm/dot_general | solution.py:23
  30.1 8.6 %fusion.109 = bf16[1,64,512,64]{2,3,0,1:T(8,128)(2,1)} fusion(f32[64,512]{1,0:T(8,128)S(1)} %convert_element_type.125, f32[4,1,64,512,64]{3,4,0,2,1:T(8,128)} %fusion.1), kind=kLoop, calls=%fused_computation.141 | loop fusion | flops 12582912 | bytes 21102592 | tf_op jit(solution)/shard_map/convert_element_type | solution.py:26
  39.6 8.6 %fusion.66 = bf16[64,512,64]{1,2,0:T(8,128)(2,1)} fusion(f32[4,1,64,512,64]{3,4,0,2,1:T(8,128)} %fusion.1, f32[64,512]{1,0:T(8,128)S(1)} %convert_element_type.125), kind=kLoop, calls=%fused_computation.88 | loop fusion | flops 12582912 | bytes 21102592 | tf_op jit(solution)/shard_map/convert_element_type | solution.py:25
  48.2 149.2 %all-gather.4.cloned.1.call-done = bf16[1,512,512,64]{2,3,0,1:T(8,128)(2,1)} async-done(((bf16[1,64,512,64]{2,3,0,1:T(8,128)(2,1)}), bf16[1,512,512,64]{2,3,0,1:T(8,128)(2,1)}) %all-gather.4.cloned.1.call-update) | async-done | bytes 33554448 | tf_op jit(solution)/shard_map/all_gather | solution.py:27
  197.4 38.3 %bitcast_reduce_fusion.1 = (f32[64,512]{1,0:T(8,128)S(1)}, f32[64,512,64]{1,2,0:T(8,128)}) fusion(bf16[64,512,64]{1,2,0:T(8,128)(2,1)} %fusion.66, bf16[1,512,512,64]{2,3,0,1:T(8,128)(2,1)} %all-gather.4.cloned.1.call-done), kind=kOutput, calls=%fused_computation.110 | convolution fusion | flops 2149548032 | bytes 46268416 | tf_op jit(solution)/shard_map/sikc,sjkc->sijc/dot_general | solution.py:28
  235.8 4.7 multiply_reduce_fusion.3
  241.5 2.2 fusion.82
  243.8 5.5 fusion.97
  249.3 5.6 convert_reduce_fusion.2
  254.9 2.0 copy-done.7
  258.6 12.4 %convert_reduce_fusion.1 = (f32[64,512]{1,0:T(8,128)S(1)}, bf16[1,64,512,64]{2,3,1,0:T(8,128)(2,1)}) fusion(f32[64]{0:T(128)S(1)} %get-tuple-element.26, bf16[2,128,64]{1,2,0:T(8,128)(2,1)S(1)} %copy-done.20, f32[128]{0:T(128)S(1)} %get-tuple-element.24, bf16[1,64,512,64]{2,3,1,0:T(8,128)(2,1)} %copy-done.7, f32[64]{0:T(128)S(1)} %get-tuple-element.10, ...), kind=kOutput, calls=%fused_computation.26 | convolution fusion | flops 1111457792 | bytes 13010944 | tf_op jit(solution)/shard_map/dot_general | solution.py:34
  271.0 3.9 fusion.32
  274.9 15.9 %fusion = f32[4,1,64,512,64]{3,4,2,1,0:T(8,128)} fusion(f32[4,64]{1,0:T(4,128)S(1)} %get-tuple-element.7, bf16[1,64,4,64]{1,3,2,0:T(8,128)(2,1)S(1)} %copy.106, bf16[1,64,512,64]{2,3,1,0:T(8,128)(2,1)} %get-tuple-element.36, f32[64]{0:T(128)S(1)} %get-tuple-element.20, f32[64]{0:T(128)S(1)} %get-tuple-element.17, f32[64,512]{1,0:T(8,128)S(1)} %add_rsqrt_fusion.3, ...), kind=kOutput, calls=%fused_computation.1 | convolution fusion | flops 1094713344 | bytes 38045184 | tf_op jit(solution)/shard_map/sikc,cgm->gsikm/dot_general | solution.py:23
  290.8 8.6 %fusion.110 = bf16[1,64,512,64]{2,3,0,1:T(8,128)(2,1)} fusion(f32[64,512]{1,0:T(8,128)S(1)} %convert_element_type.125, f32[4,1,64,512,64]{3,4,2,1,0:T(8,128)} %fusion), kind=kLoop, calls=%fused_computation.142 | loop fusion | flops 12582912 | bytes 21102592 | tf_op jit(solution)/shard_map/convert_element_type | solution.py:26
  299.6 9.0 %fusion.54 = bf16[64,512,64]{1,2,0:T(8,128)(2,1)} fusion(f32[4,1,64,512,64]{3,4,2,1,0:T(8,128)} %fusion, f32[64,512]{1,0:T(8,128)S(1)} %convert_element_type.125), kind=kLoop, calls=%fused_computation.72 | loop fusion | flops 12582912 | bytes 21102592 | tf_op jit(solution)/shard_map/convert_element_type | solution.py:25
  308.5 146.2 %all-gather.6.cloned.1.call-done = bf16[1,512,512,64]{2,3,0,1:T(8,128)(2,1)} async-done(((bf16[1,64,512,64]{2,3,0,1:T(8,128)(2,1)}), bf16[1,512,512,64]{2,3,0,1:T(8,128)(2,1)}) %all-gather.6.cloned.1.call-update) | async-done | bytes 33554448 | tf_op jit(solution)/shard_map/all_gather | solution.py:27
  454.8 38.4 %bitcast_reduce_fusion = (f32[64,512]{1,0:T(8,128)S(1)}, f32[64,512,64]{1,2,0:T(8,128)}) fusion(bf16[64,512,64]{1,2,0:T(8,128)(2,1)} %fusion.54, bf16[1,512,512,64]{2,3,0,1:T(8,128)(2,1)} %all-gather.6.cloned.1.call-done), kind=kOutput, calls=%fused_computation.108 | convolution fusion | flops 2149548032 | bytes 46268416 | tf_op jit(solution)/shard_map/sikc,sjkc->sijc/dot_general | solution.py:28
  493.2 4.7 multiply_reduce_fusion.2
  498.9 2.2 fusion.83
  501.2 5.5 fusion.94
  506.6 5.6 convert_reduce_fusion
  512.3 2.0 copy-done.6
  516.0 12.4 %convert_reduce_fusion.4 = (f32[64,512]{1,0:T(8,128)S(1)}, bf16[1,64,512,64]{2,3,1,0:T(8,128)(2,1)}) fusion(f32[64]{0:T(128)S(1)} %get-tuple-element.25, bf16[2,128,64]{1,2,0:T(8,128)(2,1)S(1)} %copy-done.20, f32[128]{0:T(128)S(1)} %get-tuple-element.23, bf16[1,64,512,64]{2,3,1,0:T(8,128)(2,1)} %copy-done.6, f32[64]{0:T(128)S(1)} %get-tuple-element.12, ...), kind=kOutput, calls=%fused_computation.34 | convolution fusion | flops 1111457792 | bytes 13010944 | tf_op jit(solution)/shard_map/dot_general | solution.py:34
  528.4 3.9 fusion.44
  532.3 6.2 fusion.47
  538.7 9.8 %convert_convert_fusion = f32[64,512,4,16]{1,3,2,0:T(8,128)} fusion(bf16[64,512,128]{2,1,0:T(8,128)(2,1)} %param.25, bf16[128,4,16]{0,2,1:T(8,128)(2,1)S(1)} %copy-done.10), kind=kOutput, calls=%fused_computation.140 | convolution fusion | flops 541065216 | bytes 16793600 | tf_op jit(solution)/shard_map/ijc,chd->ijhd/dot_general | solution.py:40
  548.5 143.0 %all-gather.8.cloned.1.call-done = bf16[4,64,512,64]{2,3,1,0:T(8,128)(2,1)} async-done(((bf16[1,64,512,64]{2,3,1,0:T(8,128)(2,1)}), bf16[4,64,512,64]{2,3,1,0:T(8,128)(2,1)}) %all-gather.8.cloned.1.call-update) | async-done | bytes 16777232 | tf_op jit(solution)/shard_map/all_gather | solution.py:62
  691.4 14.0 %multiply_reduce_fusion.1 = f32[64,512,4,4]{1,2,0,3:T(4,128)S(1)} fusion(f32[64,512,4,16]{1,3,2,0:T(8,128)} %convert_convert_fusion, bf16[4,64,512,64]{2,3,1,0:T(8,128)(2,1)} %all-gather.8.cloned.1.call-done, bf16[64,4,16]{0,2,1:T(8,128)(2,1)S(1)} %copy-done.11), kind=kOutput, calls=%fused_computation.9 | convolution fusion | flops 1106771968 | bytes 27271168 | tf_op jit(solution)/shard_map/sijc,chd->sijhd/dot_general | solution.py:41
  709.3 12.6 %multiply_reduce_fusion = bf16[64,512,4,16]{1,3,2,0:T(8,128)(2,1)} fusion(f32[64,512,4,4]{1,2,0,3:T(4,128)S(1)} %copy.108, bf16[4,64,512,64]{2,3,1,0:T(8,128)(2,1)} %all-gather.8.cloned.1.call-done, bf16[64,4,16]{0,2,1:T(8,128)(2,1)S(1)} %copy-done.22), kind=kOutput, calls=%fused_computation.8 | convolution fusion | flops 1105199104 | bytes 23076864 | tf_op jit(solution)/shard_map/sijc,chd->sijhd/dot_general | solution.py:42
  721.9 10.5 %fusion.9 = bf16[64,512,128]{2,1,0:T(8,128)(2,1)} fusion(bf16[64,512,128]{2,1,0:T(8,128)(2,1)} %param.25, f32[128]{0:T(128)S(1)} %copy-done.24, bf16[64,512,4,16]{1,3,2,0:T(8,128)(2,1)} %multiply_reduce_fusion, bf16[4,16,128]{2,1,0:T(8,128)(2,1)S(1)} %copy-done), kind=kOutput, calls=%fused_computation.14 | convolution fusion | flops 553648128 | bytes 20988416 | tf_op jit(solution)/shard_map/ijhd,hdc->ijc/dot_general | solution.py:47
  (87 shorter events, 13.2 us)
Async XLA Ops:
  6.5 715.4 %copy-start = (bf16[4,16,128]{2,1,0:T(8,128)(2,1)S(1)}, bf16[4,16,128]{2,1,0:T(8,128)(2,1)}, u32[]{:S(2)}) copy-start(bf16[4,16,128]{2,1,0:T(8,128)(2,1)} %param.44) | copy-start | bytes 49156
  6.6 10.1 %copy-start.8 = (s32[64,512]{1,0:T(8,128)S(1)}, s32[64,512]{1,0:T(8,128)}, u32[]{:S(2)}) copy-start(s32[64,512]{1,0:T(8,128)} %param.26) | copy-start | bytes 393220
  6.6 190.9 %all-gather.4.cloned.1.call-start = ((), (), s32[]{:S(2)}) async-start(), calls=%async_computation | async-start | bytes 37748736 | tf_op jit(solution)/shard_map/all_gather | solution.py:27
  8.3 8.4 %copy-start.1 = (bf16[1,64,512,64]{2,3,1,0:T(8,128)(2,1)S(1)}, bf16[1,64,512,64]{2,3,1,0:T(8,128)(2,1)}, u32[]{:S(2)}) copy-start(bf16[1,64,512,64]{2,3,1,0:T(8,128)(2,1)} %param.23) | copy-start | bytes 12582916
  30.0 9.4 %copy-start.14 = (f32[2,64]{1,0:T(2,128)S(1)}, f32[2,64]{1,0:T(2,128)}, u32[]{:S(2)}) copy-start(f32[2,64]{1,0:T(2,128)} %param.39) | copy-start | bytes 1540
  30.0 9.5 %copy-start.15 = (f32[2,128]{1,0:T(2,128)S(1)}, f32[2,128]{1,0:T(2,128)}, u32[]{:S(2)}) copy-start(f32[2,128]{1,0:T(2,128)} %param.37) | copy-start | bytes 3076
  30.0 9.5 %copy-start.12 = (f32[2,2,64]{2,1,0:T(2,128)S(1)}, f32[2,2,64]{2,1,0:T(2,128)}, u32[]{:S(2)}) copy-start(f32[2,2,64]{2,1,0:T(2,128)} %param.32) | copy-start | bytes 3076
  30.0 9.5 %copy-start.13 = (f32[2,2,64]{2,1,0:T(2,128)S(1)}, f32[2,2,64]{2,1,0:T(2,128)}, u32[]{:S(2)}) copy-start(f32[2,2,64]{2,1,0:T(2,128)} %param.35) | copy-start | bytes 3076
  30.0 9.5 %copy-start.17 = (f32[2,64]{1,0:T(2,128)S(1)}, f32[2,64]{1,0:T(2,128)}, u32[]{:S(2)}) copy-start(f32[2,64]{1,0:T(2,128)} %param.34) | copy-start | bytes 1540
  30.0 9.5 %copy-start.18 = (f32[2,64]{1,0:T(2,128)S(1)}, f32[2,64]{1,0:T(2,128)}, u32[]{:S(2)}) copy-start(f32[2,64]{1,0:T(2,128)} %param.31) | copy-start | bytes 1540
  38.7 416.0 %all-gather.6.cloned.1.call-start = ((), (), s32[]{:S(2)}) async-start(), calls=%async_computation.1 | async-start | bytes 37748736 | tf_op jit(solution)/shard_map/all_gather | solution.py:27
  235.8 5.8 copy-start.4
  240.5 3.3 copy-start.9
  243.8 5.5 copy-start.2
  243.8 5.5 copy-start.19
  249.3 9.3 %copy-start.20 = (bf16[2,128,64]{1,2,0:T(8,128)(2,1)S(1)}, bf16[2,128,64]{1,2,0:T(8,128)(2,1)}, u32[]{:S(2)}) copy-start(bf16[2,128,64]{1,2,0:T(8,128)(2,1)} %param.38) | copy-start | bytes 98308
  249.3 9.3 %copy-start.21 = (bf16[2,64,128]{2,1,0:T(8,128)(2,1)S(1)}, bf16[2,64,128]{2,1,0:T(8,128)(2,1)}, u32[]{:S(2)}) copy-start(bf16[2,64,128]{2,1,0:T(8,128)(2,1)} %param.36) | copy-start | bytes 98308
  254.9 2.0 copy-start.7
  290.8 8.7 %copy-start.16 = (f32[2,64]{1,0:T(2,128)S(1)}, f32[2,64]{1,0:T(2,128)}, u32[]{:S(2)}) copy-start(f32[2,64]{1,0:T(2,128)} %param.40) | copy-start | bytes 1540
  299.5 392.0 %all-gather.8.cloned.1.call-start = ((), (), s32[]{:S(2)}) async-start(), calls=%async_computation.2 | async-start | bytes 20971520 | tf_op jit(solution)/shard_map/all_gather | solution.py:62
  493.1 5.8 copy-start.3
  501.1 5.5 copy-start.5
  512.2 2.0 copy-start.6
  528.3 10.3 %copy-start.23 = (s32[4]{0:T(128)S(1)}, s32[4]{0:T(128)}, u32[]{:S(2)}) copy-start(s32[4]{0:T(128)} %param.24) | copy-start | bytes 52
  528.3 10.3 %copy-start.10 = (bf16[128,4,16]{0,2,1:T(8,128)(2,1)S(1)}, bf16[128,4,16]{0,2,1:T(8,128)(2,1)}, u32[]{:S(2)}) copy-start(bf16[128,4,16]{0,2,1:T(8,128)(2,1)} %param.41) | copy-start | bytes 49156
  538.7 152.8 %copy-start.11 = (bf16[64,4,16]{0,2,1:T(8,128)(2,1)S(1)}, bf16[64,4,16]{0,2,1:T(8,128)(2,1)}, u32[]{:S(2)}) copy-start(bf16[64,4,16]{0,2,1:T(8,128)(2,1)} %param.42) | copy-start | bytes 24580
  705.4 3.9 copy-start.22
  709.3 12.6 %copy-start.24 = (f32[128]{0:T(128)S(1)}, f32[128]{0:T(128)}, u32[]{:S(2)}) copy-start(f32[128]{0:T(128)} %param.45) | copy-start | bytes 1540
Sparse Core Ops, SparseCore 0:
  38.9 158.5 all-gather.3
  299.6 155.1 all-gather.5
  538.7 152.6 all-gather.7
where the time goes:
time: 746 us; the launch traced here: 740 us
  waiting for transfers between devices  439 us (59%)
  matrix products  200 us (27%)
  other arithmetic  76.1 us (10%)
  between operations  14.2 us (2%)
  local copies, waits for them, and re-layouts  10.3 us (1%)
    all_gather x2, waiting for transfers between devices, pair_block(): right_all = lax.all_gather(right_act, 'dap', axis=1, tiled=True)  295 us
    all_gather x1, waiting for transfers between devices, local_fn(): tmpl_all = lax.all_gather(tmpl_fin, 'tmpl', axis=0, tiled=True)  143 us
    dot_general x2, matrix products, pair_block(): jnp.einsum('sikc,sjkc->sijc', left_act, right_all, preferred_element_type...  76.7 us
    dot_general x2, matrix products, pair_block(): jnp.einsum('sikc,cgm->gsikm', normed, w_ab, preferred_element_type=jnp.fl...  29.2 us
    dot_general x2, matrix products, pair_block(): jnp.dot(hidden, w_down, preferred_element_type=jnp.float32) + b_down  24.7 us
    reduce_sum x7, other arithmetic, layer_norm(): row_var = jnp.mean(centered * centered, axis=-1, keepdims=True)  24.3 us
    convert_element_type x2, other arithmetic, pair_block(): (jax.nn.sigmoid(proj_all[0]) * proj_all[1] * mask_f).astype(jnp.bfloat16)  17.6 us
    convert_element_type x2, other arithmetic, pair_block(): (jax.nn.sigmoid(proj_all[2]) * proj_all[3] * mask_f).astype(jnp.bfloat16)  17.2 us
  transfers between devices with their start and end apart: 3, of which 3 were waited for; matrix products, arithmetic and copies ran while one was open for 4% of the time, Pallas kernels for 0%

commit v1 on v0

v1 whole, which is shorter than its diff:
```python
import functools
import jax
import jax.numpy as jnp
from jax import lax
from jax.experimental import pallas as pl
from jax.experimental.pallas import tpu as pltpu
from jax.sharding import PartitionSpec as P

LN_EPS = 1e-5
MASK_BIAS = 1e9
BLOCK_ARGS = 13
F32, BF16 = jnp.float32, jnp.bfloat16
NQ = 2
IB = 16
GB = 8
CB = 8
LANES = 128
PAIR_GROUP = 4
HEAD_GROUP = 4
CORES = 2


def dot(lhs, rhs, lhs_dim=1, rhs_dim=0):
    return lax.dot_general(lhs, rhs, (((lhs_dim,), (rhs_dim,)), ((), ())), preferred_element_type=F32)


def wide(param, width):
    return jnp.concatenate([param] * (width // LANES), axis=-1)


def norm_lead(val, gain, bias):
    width = val.shape[-1]
    mean = jnp.mean(val, axis=0, keepdims=True)
    cen = val - mean
    var = jnp.mean(cen * cen, axis=0, keepdims=True)
    return (cen * lax.rsqrt(var + LN_EPS) * wide(gain, width) + wide(bias, width)).astype(BF16)


def project(normed, w_ab, b_ab, mask_row):
    proj = dot(w_ab, normed) + wide(b_ab, normed.shape[-1])
    ch = proj.shape[0] // 4
    left = (jnp.tanh(proj[:ch]) + 1.0) * proj[ch:2 * ch] * mask_row
    right = (jnp.tanh(proj[2 * ch:3 * ch]) + 1.0) * proj[3 * ch:] * mask_row
    return left, right


def put_row(scr, row, rows, block, val):
    for lb in range(val.shape[1] // LANES):
        scr[block + lb, pl.ds(row, val.shape[0], stride=rows), :] = val[:, lb * LANES:(lb + 1) * LANES]


def flush(scr, out_ref):
    ch, rows, width = out_ref.shape
    for lb in range(width // LANES):
        out_ref[:, :, lb * LANES:(lb + 1) * LANES] = scr[lb].reshape(ch, rows, LANES).astype(BF16)


def head_kernel(t_ref, mask_ref, perm_ref, par_ref, wab_ref, *refs):
    a_ref, b_ref, u_ref, tt_ref, a_scr, b_scr = refs[-6:]
    rows, ch, cols = t_ref.shape
    wid = cols // NQ
    off_ln, off_ab = 0, 2 * ch
    ordered = dot(t_ref[...].reshape(rows * ch, cols), perm_ref[...])
    tt_ref[...] = ordered.astype(BF16).reshape(rows, ch, cols)
    for q in range(NQ):
        lane = slice(q * wid, (q + 1) * wid)
        for g in range(0, rows, HEAD_GROUP):
            rng = range(g, g + HEAD_GROUP)
            val = jnp.concatenate([tt_ref[r, :, lane] for r in rng], axis=1).astype(F32)
            normed = norm_lead(val, par_ref[off_ln:off_ln + ch], par_ref[off_ln + ch:off_ln + 2 * ch])
            mask_all = jnp.concatenate([mask_ref[r:r + 1, lane] for r in rng], axis=1)
            left, right = project(normed, wab_ref[...], par_ref[off_ab:off_ab + 4 * ch], mask_all)
            for n, r in enumerate(rng):
                part = slice(n * wid, (n + 1) * wid)
                u_ref[r, :, lane] = normed[:, part]
                put_row(a_scr, r, rows, q * wid // LANES, left[:, part])
                put_row(b_scr, r, rows, q * wid // LANES, right[:, part])
    flush(a_scr, a_ref)
    flush(b_scr, b_ref)


def pair_kernel(steps, na, sources, last, order_ref, *refs):
    refs = list(refs)
    a_refs, refs = refs[:na], refs[na:]
    b_refs = []
    for count in sources:
        b_refs.append(refs[:count])
        refs = refs[count:]
    t_ref, u_ref, mask_ref, lnx_ref, wmix_ref, wgate_ref, wup_ref, wdown_ref, par_ref = refs[:9]
    refs = refs[9:]
    if last:
        out_ref, x_scr = refs[:2]
        g_scrs = refs[2:]
    else:
        wab_ref, t_out, u_out, a_out = refs[:4]
        g_scrs = refs[-len(sources):]
        x_scr, a_scr, b_scr = refs[-len(sources) - 3:-len(sources)]
        b_outs = refs[4:-len(sources) - 3]
    step = pl.program_id(0)
    ch = t_ref.shape[1]
    rows, wid = IB, t_ref.shape[2]

    @pl.when(step < steps)
    def _():
        for c in range(CB):
            for g_scr, part in zip(g_scrs, b_refs):
                sub = part[0].shape[1]
                for n, b_ref in enumerate(part):
                    g_scr[c, pl.ds(pl.multiple_of(order_ref[n] * sub, sub), sub), :] = b_ref[c]
            acc = None
            for a_ref, g_scr in zip(a_refs, g_scrs):
                term = dot(a_ref[c], g_scr[c], 1, 1)
                acc = term if acc is None else acc + term
            x_scr[step * CB + c] = acc

    @pl.when(step >= steps)
    def _():
        base = (step - steps) * rows
        par = lambda n, size=1: par_ref[n * ch:(n + size) * ch, :]
        for g in range(rows // GB):
            val = x_scr[:, pl.ds(pl.multiple_of(base + g * GB, GB), GB), :]
            mixed = norm_lead(val, lnx_ref[0], lnx_ref[1]).reshape(ch * GB, wid)
            upd8 = dot(wmix_ref[...], mixed).reshape(GB, ch, wid)
            for h in range(0, GB, PAIR_GROUP):
                rng = range(g * GB + h, g * GB + h + PAIR_GROUP)
                u_all = jnp.concatenate([u_ref[r] for r in rng], axis=1)
                t_all = jnp.concatenate([t_ref[r] for r in rng], axis=1).astype(F32)
                upd = jnp.concatenate([upd8[h + n] for n in range(PAIR_GROUP)], axis=1)
                full = PAIR_GROUP * wid
                gate = jnp.tanh(dot(wgate_ref[...], u_all) + wide(par(0), full)) + 1.0
                t_all = (t_all + gate * (upd + wide(par(1), full))).astype(BF16)
                normed = norm_lead(t_all.astype(F32), par(3), par(4))
                hidden = jnp.maximum(dot(wup_ref[...], normed) + wide(par(7, 2), full), 0.0).astype(BF16)
                upd = dot(wdown_ref[...], hidden) + wide(par(2), full)
                t_all = (t_all.astype(F32) + upd).astype(BF16)
                normed = norm_lead(t_all.astype(F32), par(5), par(6))
                if last:
                    for n, r in enumerate(rng):
                        out_ref[r] = normed[:, n * wid:(n + 1) * wid]
                else:
                    mask_all = jnp.concatenate([mask_ref[r:r + 1, :] for r in rng], axis=1)
                    left, right = project(normed, wab_ref[...], par(9, 4), mask_all)
                    for n, r in enumerate(rng):
                        cols = slice(n * wid, (n + 1) * wid)
                        t_out[r] = t_all[:, cols]
                        u_out[r] = normed[:, cols]
                        put_row(a_scr, r, rows, 0, left[:, cols])
                        put_row(b_scr, r, rows, 0, right[:, cols])
        if not last:
            flush(a_scr, a_out)
            if len(b_outs) == 1:
                flush(b_scr, b_outs[0])
            else:
                per = pl.num_programs(0) - steps
                for n, b_out in enumerate(b_outs):
                    here = (step - steps) // (per // len(b_outs)) == n
                    pl.when(here)(functools.partial(flush, b_scr, b_out))


def attend_kernel(heads, bias_ref, t_ref, z_ref, wq_ref, wkv_ref, o_ref):
    num, rows, _, wid = t_ref.shape
    dim = wq_ref.shape[0] // heads

    def one_row(row, carry):
        zed = z_ref[row].reshape(wid, -1)
        query = dot(wq_ref[...], zed, 1, 1).astype(BF16).astype(F32)
        logits, values = [], []
        for s in range(num):
            kv = dot(wkv_ref[...], t_ref[s, row]).astype(BF16).astype(F32)
            half = kv.shape[0] // 2
            values.append(kv[half:].reshape(heads, dim, wid))
            score = jnp.sum((query * kv[:half]).reshape(heads, dim, wid), axis=1, keepdims=True)
            logits.append(score * dim ** -0.5 + bias_ref[s])
        top = functools.reduce(jnp.maximum, logits)
        exps = [jnp.exp(lg - top) for lg in logits]
        total = functools.reduce(jnp.add, exps)
        out = None
        for s in range(num):
            term = (exps[s] / total).astype(BF16).astype(F32) * values[s]
            out = term if out is None else out + term
        o_ref[row] = out.reshape(heads * dim, wid).astype(BF16)
        return carry

    lax.fori_loop(0, rows, one_row, 0)


def out_kernel(num, per_part, _, *refs):
    o_refs, (z_ref, w_ref, b_ref) = refs[:num], refs[num:num + 3]
    y_ref = refs[-1]
    rows, dap, sub, width = z_ref.shape
    for n, o_ref in enumerate(o_refs):
        @pl.when(pl.program_id(0) // per_part == n)
        def _(o_ref=o_ref):
            for row in range(rows):
                upd = dot(o_ref[row], w_ref[...], 0, 0) + b_ref[...]
                y_ref[row] = (z_ref[row].astype(F32) + upd.reshape(dap, sub, width)).astype(BF16)


def whole(arr):
    return pl.BlockSpec(arr.shape, lambda *_: (0,) * arr.ndim)


def sds(shape, dtype=BF16):
    return jax.ShapeDtypeStruct(shape, dtype)


def cost(flops, nbytes):
    return pl.CostEstimate(flops=flops, bytes_accessed=nbytes, transcendentals=0)


def col(param):
    return jnp.broadcast_to(param[..., None], param.shape + (LANES,))


def head(t_nat, mask_f, part, perm, par, w_ab, into, after):
    rows, ch, cols = t_nat.shape
    mine = rows // NQ
    first = part * (mine // IB)
    row_block = pl.BlockSpec((IB, ch, cols), lambda s: (first + s, 0, 0))
    extra = list(into) + list(after)
    return pl.pallas_call(
        head_kernel,
        grid=(mine // IB,),
        in_specs=[row_block, pl.BlockSpec((IB, cols), lambda s: (first + s, 0)),
                  whole(perm), whole(par), whole(w_ab)] + [pl.BlockSpec(memory_space=pl.ANY)] * len(extra),
        out_specs=[pl.BlockSpec((ch, IB, cols), lambda s: (0, first + s, 0)),
                   pl.BlockSpec((ch, IB, cols), lambda s: (0, s, 0)), row_block, row_block],
        out_shape=[sds((ch, rows, cols)), sds((ch, mine, cols)), sds((rows, ch, cols)), sds((rows, ch, cols))],
        input_output_aliases={5: 0, 6: 2, 7: 3} if into else {},
        scratch_shapes=[pltpu.VMEM((cols // LANES, ch * IB, LANES), F32)] * 2,
        cost_estimate=cost(2 * mine * cols * ch * 16 * ch, 5 * mine * cols * ch * 2),
    )(t_nat, mask_f, perm, par, w_ab, *extra)


def pair(q, order, a_parts, b_parts, b_index, t_arr, u_arr, mask_f, weights, next_w, split_b, last):
    ch = a_parts[0].shape[0]
    rows, cols = mask_f.shape
    wid = cols // NQ
    dap = len(b_parts[0])
    sub = wid // dap
    steps, row_steps = ch // CB, rows // IB
    tri = lambda s: jnp.minimum(s, steps - 1)
    row = lambda s: jnp.maximum(s - steps, 0)
    fixed = lambda arr: pl.BlockSpec(arr.shape, lambda s, o: (0,) * arr.ndim)
    in_specs = [pl.BlockSpec((CB,) + a.shape[1:], lambda s, o: (tri(s), 0, 0)) for a in a_parts]
    scratch_b = []
    for part, where in zip(b_parts, b_index):
        depth = part[0].shape[2]
        in_specs += [pl.BlockSpec((CB, sub, depth), lambda s, o, where=where: (tri(s), where, 0))] * dap
        scratch_b.append(pltpu.VMEM((CB, wid, depth), BF16))
    t_col = 0 if t_arr.shape[2] == wid else q
    in_specs += [pl.BlockSpec((IB, ch, wid), lambda s, o: (row(s), 0, t_col))] * 2
    in_specs += [pl.BlockSpec((IB, wid), lambda s, o: (row(s), q))]
    tail = list(weights) + list(next_w)
    in_specs += [fixed(w) for w in tail]
    scratch = [pltpu.VMEM((ch, rows, wid), F32)]
    row_out = pl.BlockSpec((IB, ch, wid), lambda s, o: (row(s), 0, 0))
    if last:
        out_shape, out_specs = [sds((rows, ch, wid))], [row_out]
    else:
        out_shape = [sds((rows, ch, wid))] * 2 + [sds((ch, rows, wid))]
        out_specs = [row_out] * 2 + [pl.BlockSpec((ch, IB, wid), lambda s, o: (0, row(s), 0))]
        per = row_steps // split_b
        for n in range(split_b):
            out_shape.append(sds((ch, rows // split_b, wid)))
            out_specs.append(pl.BlockSpec((ch, IB, wid), lambda s, o, n=n: (0, jnp.clip(row(s) - n * per, 0, per - 1), 0)))
        scratch += [pltpu.VMEM((wid // LANES, ch * IB, LANES), F32)] * 2
    flops = 2 * rows * wid * ch * (cols + 40 * ch)
    return pl.pallas_call(
        functools.partial(pair_kernel, steps, len(a_parts), [dap] * len(b_parts), last),
        grid_spec=pltpu.PrefetchScalarGridSpec(
            num_scalar_prefetch=1, grid=(steps + row_steps,), in_specs=in_specs, out_specs=out_specs,
            scratch_shapes=scratch + scratch_b),
        out_shape=out_shape,
        cost_estimate=cost(flops, 4 * rows * cols * ch),
    )(order, *a_parts, *sum(b_parts, []), t_arr, u_arr, mask_f, *tail)


def attend(q, t_all, pair_loc, bias, w_q, w_kv, heads, quarter):
    num, rows, ch, wid = t_all.shape
    _, dap, per, width = pair_loc.shape
    ib = 8
    grid_spec = pltpu.PrefetchScalarGridSpec(
        num_scalar_prefetch=1,
        grid=(rows // ib,),
        in_specs=[pl.BlockSpec(memory_space=pltpu.SMEM),
                  pl.BlockSpec((num, ib, ch, wid), lambda s, r: (0, s, 0, 0)),
                  pl.BlockSpec((ib, dap, per // NQ, width), lambda s, r: (r[0] * (rows // ib) + s, 0, q, 0)),
                  pl.BlockSpec(w_q.shape, lambda s, r: (0, 0)),
                  pl.BlockSpec(w_kv.shape, lambda s, r: (0, 0))],
        out_specs=pl.BlockSpec((ib, w_q.shape[0], wid), lambda s, r: (s, 0, 0)),
    )
    return pl.pallas_call(
        lambda r_ref, *refs: attend_kernel(heads, *refs),
        grid_spec=grid_spec,
        out_shape=sds((rows, w_q.shape[0], wid)),
        cost_estimate=cost(2 * rows * wid * (num * ch * 4 * ch + width * ch), 8 * rows * wid * ch),
    )(quarter, bias, t_all, pair_loc, w_q, w_kv)


def project_out(q, where, o_parts, pair_loc, w_out, b_out, into):
    rows, dap, per, width = pair_loc.shape
    num = len(o_parts)
    ib = 8
    per_part = rows // num // ib
    z_spec = pl.BlockSpec((ib, dap, per // NQ, width), lambda s, w: (w[s // per_part] * per_part + s % per_part, 0, q, 0))
    o_specs = [pl.BlockSpec((ib,) + o.shape[1:], lambda s, w, n=n: (jnp.clip(s - n * per_part, 0, per_part - 1), 0, 0))
               for n, o in enumerate(o_parts)]
    fixed = lambda arr: pl.BlockSpec(arr.shape, lambda s, w: (0, 0))
    extra = [] if into is None else [into]
    return pl.pallas_call(
        functools.partial(out_kernel, num, per_part),
        grid_spec=pltpu.PrefetchScalarGridSpec(
            num_scalar_prefetch=1, grid=(rows // ib,),
            in_specs=o_specs + [z_spec, fixed(w_out), fixed(b_out)] + [pl.BlockSpec(memory_space=pl.ANY)] * len(extra),
            out_specs=z_spec),
        out_shape=sds(pair_loc.shape),
        input_output_aliases={} if into is None else {num + 4: 0},
        cost_estimate=cost(4 * rows * dap * per * width * o_parts[0].shape[1] // NQ, 6 * rows * dap * per * width // NQ),
    )(where, *o_parts, pair_loc, w_out, b_out, *extra)


def mix_weights(blk):
    ln_mix, w_mix = blk[5:7]
    ch = w_mix.shape[0]
    lnx = jnp.broadcast_to(ln_mix[:, :, None, None], (2, ch, GB, LANES))
    eye = jnp.eye(GB, dtype=BF16)
    return lnx, ((w_mix.T * 0.5)[None, :, :, None] * eye[:, None, None, :]).reshape(GB * ch, ch * GB)


def block_weights(blk, par):
    w_gate, w_up, w_down = blk[3], blk[9], blk[11]
    return mix_weights(blk) + (w_gate.T * 0.5, w_up.T, w_down.T, par)


def columns(blk, fin, next_b):
    _, _, _, _, b_gate, _, _, b_mix, ln_tr, _, b_up, _, b_down = blk
    return [b_gate * 0.5, b_mix * 0.5, b_down, *ln_tr, *fin, b_up] + ([] if next_b is None else [next_b.reshape(-1) * 0.5])


def half_w_ab(w_ab):
    return w_ab.reshape(w_ab.shape[0], -1).T * 0.5


def ring_step(val, axis, size, step, cores, flip=False):
    pairs = []
    for src in range(size * cores):
        chip, core = src // cores, src % cores
        pairs.append((src, (chip + step) % size * cores + (cores - 1 - core if flip else core)))
    return lax.ppermute(val, axis, pairs)


def ring_gather(val, axis, size, cores, forward):
    back = ring_step(val, axis, size, 1, cores)
    on = ring_step(val, axis, size, -1, cores)
    far = ring_step(back if forward > 0 else on, axis, size, forward, cores)
    return [val, back, on, far]


def solution(mesh):
    tmpl_spec = P(('batch', 'tmpl'), 'dap')
    row_spec = P(('batch', 'dap'))
    dap, tmpl = mesh.shape['dap'], mesh.shape['tmpl']
    chips = dap // CORES

    def gather(part, forward):
        mine = ring_gather(part, 'dap', chips, CORES, forward)
        other = [ring_step(val, 'dap', chips, 0, CORES, True) for val in mine]
        return mine + other

    def local_fn(tmpl_loc, tmpl_mask, pair_loc, mask_loc, *weights):
        _, rows, cols, ch = tmpl_loc.shape
        blk0, blk1 = (tuple(w[i] for w in weights[:BLOCK_ARGS]) for i in range(2))
        ln_fin, w_query, w_key, w_value, w_out, b_out = weights[BLOCK_ARGS:]
        heads = w_query.shape[1]
        per = cols // dap
        sub = per // NQ
        me = lax.axis_index('dap').astype(jnp.int32)
        chip, core = me // CORES, me % CORES
        hops = jnp.array([0, -1, 1, 2], jnp.int32)
        near = (chip + hops) % chips * CORES
        order = jnp.concatenate([near + core, near + (CORES - 1 - core)])

        lane = jnp.arange(cols, dtype=jnp.int32)
        source = lane // sub % dap * per + lane // (dap * sub) * sub + lane % sub
        perm = (lane[:, None] == source[None, :]).astype(BF16)
        mask_f = mask_loc.astype(F32).reshape(rows, dap, NQ, sub).swapaxes(1, 2).reshape(rows, cols)
        t_nat = tmpl_loc.reshape(rows, cols, ch).swapaxes(1, 2)
        head_par = [*blk0[0], blk0[2].reshape(-1) * 0.5]
        pars = [head_par, columns(blk0, blk1[0], blk1[2]), columns(blk1, ln_fin, None)]
        par_head = col(jnp.concatenate(pars[0]))
        par0, par1 = col(jnp.concatenate(pars[1])), col(jnp.concatenate(pars[2]))

        first_w, next_w = block_weights(blk0, par0), (half_w_ab(blk1[1]),)
        second_w = block_weights(blk1, par1)
        w_q = w_query.reshape(w_query.shape[0], -1).T
        w_kv = jnp.concatenate([w_key.reshape(ch, -1), w_value.reshape(ch, -1)], axis=1).T

        b1, into, after = [], (), ()
        for part in range(NQ):
            a1, b, u1, t1 = head(t_nat, mask_f, part, perm, par_head, half_w_ab(blk0[1]), into, after)
            into, after = (a1, u1, t1), first_w + next_w + second_w + (w_q, w_kv)
            b1.append(gather(b, 1 if part == 0 else -1))

        t2, u2, a2, b2 = [], [], [], []
        for q in range(NQ):
            split = 1 if q < NQ - 1 else NQ
            out = pair(q, order, [a1], [b1[q]], [0], t1, u1, mask_f, first_w, next_w, split, False)
            t2.append(out[0])
            u2.append(out[1])
            a2.append(out[2])
            b2.append([gather(b, 1 if q < NQ - 1 else -1) for b in out[3:]])

        bias = MASK_BIAS * (tmpl_mask.astype(F32) - 1.0)
        z_view = pair_loc.reshape(rows, dap, per, pair_loc.shape[2])
        quarter = lax.axis_index('tmpl').astype(jnp.int32).reshape(1)
        where = (quarter + hops) % tmpl
        z_out = None
        for q in range(NQ):
            b_parts = [b2[k][0] for k in range(NQ - 1)] + [b2[NQ - 1][q]]
            fin, = pair(q, order, a2, b_parts, [q] * (NQ - 1) + [0], t2[q], u2[q], mask_f, second_w, (), 0, True)
            fin = fin.reshape(tmpl, rows // tmpl, ch, fin.shape[2])
            t_all = lax.all_to_all(fin, 'tmpl', 0, 0)
            o_loc = attend(q, t_all, z_view, bias, w_q, w_kv, heads, quarter)
            o_parts = ring_gather(o_loc, 'tmpl', tmpl, 1, 1 if q == 0 else -1)
            z_out = project_out(q, where, o_parts, z_view, w_out.reshape(-1, w_out.shape[2]), b_out[None], z_out)
        return z_out.reshape(pair_loc.shape)

    in_specs = (tmpl_spec, P('batch'), row_spec, row_spec) + (P(),) * (BLOCK_ARGS + 6)
    return jax.shard_map(local_fn, mesh=mesh, in_specs=in_specs, out_specs=row_spec, check_vma=False)
```

time: 746 us -> 528 us (0.71)
  matrix products: 200 us -> 0 us
  Pallas kernels: 0 us -> 170 us
  waiting for transfers between devices: 439 us -> 271 us
  other arithmetic: 76.1 us -> 4.31 us
  starting transfers between devices: 0.66 us -> 53.9 us
  between operations: 14.2 us -> 0.48 us
  local copies, waits for them, and re-layouts: 10.3 us -> 19.4 us
    all_gather x3 -> x0, waiting for transfers between devices: 438 us -> none  [the longest x2 295 us: pair_block(): right_all = lax.all_gather(right_act, 'dap', axis=1, tiled=True)]
    ppermute x0 -> x41, waiting for transfers between devices: none -> 254 us  [ring_step(): return lax.ppermute(val, axis, pairs)]
    dot_general x14 -> x0, matrix products: 200 us -> none  [the longest x2 76.7 us: pair_block(): jnp.einsum('sikc,sjkc->sijc', left_act, right_all, preferred_element_type...]
    pallas_call x0 -> x10, Pallas kernels: none -> 170 us  [the longest x4 115 us: pair(): pl.pallas_call(functools.partial(pair_kernel, steps, len(a_parts), [dap]...]
    ppermute x0 -> x41, starting transfers between devices: none -> 43.2 us  [ring_step(): return lax.ppermute(val, axis, pairs)]
    convert_element_type x6 -> x3, other arithmetic: 41.1 us -> 0.94 us  [the longest x1 0.91 us: local_fn(): perm = (lane[:, None] == source[None, :]).astype(BF16)]
    reduce_sum x9 -> x0, other arithmetic: 28.7 us -> none  [the longest x7 24.3 us: layer_norm(): row_var = jnp.mean(centered * centered, axis=-1, keepdims=True)]
    all_to_all x0 -> x2, waiting for transfers between devices: none -> 17.1 us  [local_fn(): t_all = lax.all_to_all(fin, 'tmpl', 0, 0)]
  transfers between devices with their start and end apart: 3 -> 43, of which waited for: 3 -> 15; matrix products, arithmetic and copies ran while one was open for 4% -> 3% of each run, Pallas kernels for 0% -> 29%
where the time goes in v1:
time: 528 us; the launch traced here: 519 us
  waiting for transfers between devices  271 us (51%)
  Pallas kernels  170 us (32%)
  starting transfers between devices  53.9 us (10%)
  local copies, waits for them, and re-layouts  19.4 us (4%)
    ppermute x41, waiting for transfers between devices, ring_step(): return lax.ppermute(val, axis, pairs)  254 us
    pallas_call x4, Pallas kernels, pair(): pl.pallas_call(functools.partial(pair_kernel, steps, len(a_parts), [dap]...  115 us
    ppermute x41, starting transfers between devices, ring_step(): return lax.ppermute(val, axis, pairs)  43.2 us
    pallas_call x2, Pallas kernels, head(): pl.pallas_call(head_kernel, grid=(mine // IB,), in_specs=[row_block, pl.B...  22.4 us
    pallas_call x2, Pallas kernels, project_out(): pl.pallas_call(functools.partial(out_kernel, num, per_part), grid_spec=pl...  18 us
    all_to_all x2, waiting for transfers between devices, local_fn(): t_all = lax.all_to_all(fin, 'tmpl', 0, 0)  17.1 us
    pallas_call x2, Pallas kernels, attend(): pl.pallas_call(lambda r_ref, *refs: attend_kernel(heads, *refs), grid_spe...  13.9 us
    all_to_all x2, starting transfers between devices, local_fn(): t_all = lax.all_to_all(fin, 'tmpl', 0, 0)  10.7 us
  transfers between devices with their start and end apart: 43, of which 15 were waited for; matrix products, arithmetic and copies ran while one was open for 3% of the time, Pallas kernels for 29%

profile of v1, /device:TPU:97, one launch (start us, length us, event | category | flops | bytes accessed | tf_op | source)
XLA Modules:
  0.0 518.8 jit_solution(16661990836893554059)
XLA Ops:
  4.7 11.2 %shard_map.226 = (bf16[64,64,512]{2,1,0:T(8,128)(2,1)}, bf16[64,32,512]{2,1,0:T(8,128)(2,1)}, bf16[64,64,512]{2,1,0:T(8,128)(2,1)}, bf16[64,64,512]{2,1,0:T(8,128)(2,1)}) custom-call(bf16[64,64,512]{2,1,0:T(8,128)(2,1)} %bitcast.111, f32[64,512]{1,0:T(8,128)} %copy.51.mask_ref.refs_11_.refs_20_, bf16[512,512]{1,0:T(8,128)(2,1)} %fusion.perm_ref, ...), custom_call_target="tpu_custom_call" | custom-call | flops 2147483648 | bytes 10485760 | tf_op jit(solution)/shard_map/pallas_call | solution.py:221
  15.9 2.3 collective-permute-start
  33.5 11.2 %shard_map.227 = (bf16[64,64,512]{2,1,0:T(8,128)(2,1)}, bf16[64,32,512]{2,1,0:T(8,128)(2,1)}, bf16[64,64,512]{2,1,0:T(8,128)(2,1)}, bf16[64,64,512]{2,1,0:T(8,128)(2,1)}) custom-call(bf16[64,64,512]{2,1,0:T(8,128)(2,1)} %bitcast.112, f32[64,512]{1,0:T(8,128)} %copy.51.mask_ref.refs_11_.refs_20_, ...), custom_call_target="tpu_custom_call", output_to_operand_aliasing={{0}: (5, {}), {2}: (6, {}), {3}: (7, {})} | custom-call | flops 2147483648 | bytes 10485760 | tf_op jit(solution)/shard_map/pallas_call | solution.py:221
  45.8 19.0 %collective-permute-done.refs_2_ = bf16[64,32,512]{2,1,0:T(8,128)(2,1)} collective-permute-done((bf16[64,32,512]{2,1,0:T(8,128)(2,1)}, bf16[64,32,512]{2,1,0:T(8,128)(2,1)}, u32[]{:S(2)}, u32[]{:S(2)}) %collective-permute-start) | collective-permute-done | bytes 2097184 | tf_op jit(solution)/shard_map/ppermute | solution.py:350
  68.5 41.2 %collective-permute-done.8.refs_3_ = bf16[64,32,512]{2,1,0:T(8,128)(2,1)} collective-permute-done((bf16[64,32,512]{2,1,0:T(8,128)(2,1)}, bf16[64,32,512]{2,1,0:T(8,128)(2,1)}, u32[]{:S(2)}, u32[]{:S(2)}) %collective-permute-start.8) | collective-permute-done | bytes 2097184 | tf_op jit(solution)/shard_map/ppermute | solution.py:350
  109.7 2.6 collective-permute-start.9
  112.3 4.2 collective-permute-start.6
  116.5 40.1 %collective-permute-done.7.refs_2_ = bf16[64,32,512]{2,1,0:T(8,128)(2,1)} collective-permute-done((bf16[64,32,512]{2,1,0:T(8,128)(2,1)}, bf16[64,32,512]{2,1,0:T(8,128)(2,1)}, u32[]{:S(2)}, u32[]{:S(2)}) %collective-permute-start.7) | collective-permute-done | bytes 2097184 | tf_op jit(solution)/shard_map/ppermute | solution.py:350
  156.7 2.6 collective-permute-start.10
  161.2 32.6 %shard_map.228 = (bf16[64,64,256]{2,1,0:T(8,128)(2,1)}, bf16[64,64,256]{2,1,0:T(8,128)(2,1)}, bf16[64,64,256]{2,1,0:T(8,128)(2,1)}, bf16[64,64,256]{2,1,0:T(8,128)(2,1)}) custom-call(s32[8]{0:T(128)} %pad_add_fusion.order_ref, bf16[64,64,512]{2,1,0:T(8,128)(2,1)} %get-tuple-element.25.refs_0_, bf16[64,32,512]{2,1,0:T(8,128)(2,1)} %get-tuple-element.26.refs_1_, ...), custom_call_target="tpu_custom_call" | custom-call | flops 6442450944 | bytes 8388608 | tf_op jit(solution)/shard_map/pallas_call | solution.py:269
  194.0 33.2 %shard_map.229 = (bf16[64,64,256]{2,1,0:T(8,128)(2,1)}, bf16[64,64,256]{2,1,0:T(8,128)(2,1)}, bf16[64,64,256]{2,1,0:T(8,128)(2,1)}, bf16[64,32,256]{2,1,0:T(8,128)(2,1)}, bf16[64,32,256]{2,1,0:T(8,128)(2,1)}) custom-call(s32[8]{0:T(128)} %pad_add_fusion.order_ref, bf16[64,64,512]{2,1,0:T(8,128)(2,1)} %get-tuple-element.25.refs_0_, ...), custom_call_target="tpu_custom_call" | custom-call | flops 6442450944 | bytes 8388608 | tf_op jit(solution)/shard_map/pallas_call | solution.py:269
  227.6 2.3 collective-permute-start.22
  229.9 2.7 collective-permute-start.32
  232.6 32.0 %collective-permute-done.21.refs_11_ = bf16[64,32,256]{2,1,0:T(8,128)(2,1)S(1)} collective-permute-done((bf16[64,32,256]{2,1,0:T(8,128)(2,1)}, bf16[64,32,256]{2,1,0:T(8,128)(2,1)S(1)}, u32[]{:S(2)}, u32[]{:S(2)}) %collective-permute-start.21) | collective-permute-done | bytes 1048608 | tf_op jit(solution)/shard_map/ppermute | solution.py:350
  264.6 2.1 collective-permute-start.34
  268.2 18.8 %collective-permute-done.31.refs_11_ = bf16[64,32,256]{2,1,0:T(8,128)(2,1)S(1)} collective-permute-done((bf16[64,32,256]{2,1,0:T(8,128)(2,1)}, bf16[64,32,256]{2,1,0:T(8,128)(2,1)S(1)}, u32[]{:S(2)}, u32[]{:S(2)}) %collective-permute-start.31) | collective-permute-done | bytes 1048608 | tf_op jit(solution)/shard_map/ppermute | solution.py:350
  290.2 53.0 %collective-permute-done.23.refs_13_ = bf16[64,32,256]{2,1,0:T(8,128)(2,1)} collective-permute-done((bf16[64,32,256]{2,1,0:T(8,128)(2,1)}, bf16[64,32,256]{2,1,0:T(8,128)(2,1)}, u32[]{:S(2)}, u32[]{:S(2)}) %collective-permute-start.23) | collective-permute-done | bytes 1048608 | tf_op jit(solution)/shard_map/ppermute | solution.py:350
  345.0 20.5 %collective-permute-done.33.refs_13_ = bf16[64,32,256]{2,1,0:T(8,128)(2,1)S(1)} collective-permute-done((bf16[64,32,256]{2,1,0:T(8,128)(2,1)S(1)}, bf16[64,32,256]{2,1,0:T(8,128)(2,1)S(1)}, u32[]{:S(2)}, u32[]{:S(2)}) %collective-permute-start.33) | collective-permute-done | bytes 1048608 | tf_op jit(solution)/shard_map/ppermute | solution.py:350
  369.5 9.9 %collective-permute-done.37.refs_17_ = bf16[64,32,256]{2,1,0:T(8,128)(2,1)S(1)} collective-permute-done((bf16[64,32,256]{2,1,0:T(8,128)(2,1)S(1)}, bf16[64,32,256]{2,1,0:T(8,128)(2,1)S(1)}, u32[]{:S(2)}, u32[]{:S(2)}) %collective-permute-start.37) | collective-permute-done | bytes 1048608 | tf_op jit(solution)/shard_map/ppermute | solution.py:350
  382.5 24.8 %shard_map.232 = bf16[64,64,256]{2,1,0:T(8,128)(2,1)} custom-call(s32[8]{0:T(128)} %pad_add_fusion.order_ref, bf16[64,64,256]{2,1,0:T(8,128)(2,1)} %get-tuple-element.29.refs_0_, bf16[64,64,256]{2,1,0:T(8,128)(2,1)} %get-tuple-element.31.refs_1_, bf16[64,64,256]{2,1,0:T(8,128)(2,1)} %get-tuple-element.32.refs_2_, ...), custom_call_target="tpu_custom_call" | custom-call | flops 6442450944 | bytes 8388608 | tf_op jit(solution)/shard_map/pallas_call | solution.py:269
  407.3 6.2 %all-to-all-start.1 = ((bf16[4,16,64,256]{3,2,1,0:T(8,128)(2,1)}), bf16[4,16,64,256]{3,2,1,0:T(8,128)(2,1)S(1)}, u32[]{:S(2)}, u32[]{:S(2)}) async-start(bf16[4,16,64,256]{3,2,1,0:T(8,128)(2,1)} %bitcast.109), calls=%async_computation.1 | async-start | bytes 4194304 | tf_op jit(solution)/shard_map/all_to_all | solution.py:423
  413.5 24.8 %shard_map.230 = bf16[64,64,256]{2,1,0:T(8,128)(2,1)} custom-call(s32[8]{0:T(128)} %pad_add_fusion.order_ref, bf16[64,64,256]{2,1,0:T(8,128)(2,1)} %get-tuple-element.29.refs_0_, bf16[64,64,256]{2,1,0:T(8,128)(2,1)} %get-tuple-element.31.refs_1_, bf16[64,64,256]{2,1,0:T(8,128)(2,1)} %get-tuple-element.32.refs_2_, ...), custom_call_target="tpu_custom_call" | custom-call | flops 6442450944 | bytes 8388608 | tf_op jit(solution)/shard_map/pallas_call | solution.py:269
  440.6 4.5 all-to-all-start
  445.7 7.0 %shard_map.233.refs_0_ = bf16[16,64,256]{2,1,0:T(8,128)(2,1)} custom-call(s32[1]{0:T(128)} %bitcast.r_ref, f32[4]{0:T(128)} %add_multiply_fusion.refs_0_, bf16[4,16,64,256]{3,2,1,0:T(8,128)(2,1)} %copy-done.7, bf16[64,8,64,128]{3,2,1,0:T(8,128)(2,1)} %bitcast.105, bf16[64,128]{1,0:T(8,128)(2,1)} %bitcast.127, ...), custom_call_target="tpu_custom_call" | custom-call | flops 603979776 | bytes 2097152 | tf_op jit(solution)/shard_map/pallas_call | solution.py:293
  454.0 16.1 %all-to-all-done.refs_1_ = bf16[4,16,64,256]{3,2,1,0:T(8,128)(2,1)} async-done(((bf16[4,16,64,256]{3,2,1,0:T(8,128)(2,1)}), bf16[4,16,64,256]{3,2,1,0:T(8,128)(2,1)}, u32[]{:S(2)}, u32[]{:S(2)}) %all-to-all-start) | async-done | bytes 2097184 | tf_op jit(solution)/shard_map/all_to_all | solution.py:423
  470.2 6.9 %shard_map.231.refs_0_ = bf16[16,64,256]{2,1,0:T(8,128)(2,1)} custom-call(s32[1]{0:T(128)} %bitcast.r_ref, f32[4]{0:T(128)} %add_multiply_fusion.refs_0_, bf16[4,16,64,256]{3,2,1,0:T(8,128)(2,1)} %all-to-all-done.refs_1_, bf16[64,8,64,128]{3,2,1,0:T(8,128)(2,1)} %bitcast.106, bf16[64,128]{1,0:T(8,128)(2,1)} %bitcast.128, ...), custom_call_target="tpu_custom_call" | custom-call | flops 603979776 | bytes 2097152 | tf_op jit(solution)/shard_map/pallas_call | solution.py:293
  478.0 2.9 collective-permute-done.38.refs_1_
  481.2 5.3 %collective-permute-done.29.refs_2_ = bf16[16,64,256]{2,1,0:T(8,128)(2,1)S(1)} collective-permute-done((bf16[16,64,256]{2,1,0:T(8,128)(2,1)}, bf16[16,64,256]{2,1,0:T(8,128)(2,1)S(1)}, u32[]{:S(2)}, u32[]{:S(2)}) %collective-permute-start.29) | collective-permute-done | bytes 524320 | tf_op jit(solution)/shard_map/ppermute | solution.py:350
  486.5 3.1 collective-permute-start.30
  489.7 8.1 %collective-permute-done.39.refs_2_ = bf16[16,64,256]{2,1,0:T(8,128)(2,1)S(1)} collective-permute-done((bf16[16,64,256]{2,1,0:T(8,128)(2,1)S(1)}, bf16[16,64,256]{2,1,0:T(8,128)(2,1)S(1)}, u32[]{:S(2)}, u32[]{:S(2)}) %collective-permute-start.39) | collective-permute-done | bytes 524320 | tf_op jit(solution)/shard_map/ppermute | solution.py:350
  498.7 9.0 %shard_map.234.refs_7_ = bf16[64,8,64,128]{3,2,1,0:T(8,128)(2,1)} custom-call(s32[4]{0:T(128)} %get-tuple-element.75._, bf16[16,64,256]{2,1,0:T(8,128)(2,1)} %shard_map.233.refs_0_, bf16[16,64,256]{2,1,0:T(8,128)(2,1)} %copy-done.17, bf16[16,64,256]{2,1,0:T(8,128)(2,1)} %copy-done.20, bf16[16,64,256]{2,1,0:T(8,128)(2,1)} %copy-done.22, ...), custom_call_target="tpu_custom_call" | custom-call | flops 536870912 | bytes 12582912 | tf_op jit(solution)/shard_map/pallas_call | solution.py:311
  509.8 9.0 %shard_map.235 = bf16[64,8,64,128]{3,2,1,0:T(8,128)(2,1)} custom-call(s32[4]{0:T(128)} %get-tuple-element.75._, bf16[16,64,256]{2,1,0:T(8,128)(2,1)} %shard_map.231.refs_0_, bf16[16,64,256]{2,1,0:T(8,128)(2,1)} %copy-done.19, bf16[16,64,256]{2,1,0:T(8,128)(2,1)} %copy-done.18, bf16[16,64,256]{2,1,0:T(8,128)(2,1)} %copy-done.21, ...), custom_call_target="tpu_custom_call", output_to_operand_aliasing={{}: (8, {})} | custom-call | flops 536870912 | bytes 12582912 | tf_op jit(solution)/shard_map/pallas_call | solution.py:311
  (197 shorter events, 48.8 us)
Async XLA Ops:
  15.9 48.9 %collective-permute-start = (bf16[64,32,512]{2,1,0:T(8,128)(2,1)}, bf16[64,32,512]{2,1,0:T(8,128)(2,1)}, u32[]{:S(2)}, u32[]{:S(2)}) collective-permute-start(bf16[64,32,512]{2,1,0:T(8,128)(2,1)} %get-tuple-element.26.refs_1_), channel_id=1, source_target_pairs={{0,2},{1,3},{2,4},{3,5},{4,6},{5,7},{6,0},{7,1},{8,10},{9,11},{10,... | collective-permute-start | bytes 6291464 | tf_op jit(solution)/shard_map/ppermute | solution.py:350
  18.1 48.2 %collective-permute-start.1 = (bf16[64,32,512]{2,1,0:T(8,128)(2,1)}, bf16[64,32,512]{2,1,0:T(8,128)(2,1)}, u32[]{:S(2)}, u32[]{:S(2)}) collective-permute-start(bf16[64,32,512]{2,1,0:T(8,128)(2,1)} %get-tuple-element.26.refs_1_), channel_id=1, source_target_pairs={{0,6},{1,7},{2,0},{3,1},{4,2},{5,3},{6,4},{7,5},{8,14},{9,15},{10,... | collective-permute-start | bytes 6291464 | tf_op jit(solution)/shard_map/ppermute | solution.py:350
  19.8 48.6 %collective-permute-start.3 = (bf16[64,32,512]{2,1,0:T(8,128)(2,1)}, bf16[64,32,512]{2,1,0:T(8,128)(2,1)}, u32[]{:S(2)}, u32[]{:S(2)}) collective-permute-start(bf16[64,32,512]{2,1,0:T(8,128)(2,1)} %get-tuple-element.26.refs_1_), channel_id=1, source_target_pairs={{0,1},{1,0},{2,3},{3,2},{4,5},{5,4},{6,7},{7,6},{8,9},{9,8},{10,11... | collective-permute-start | bytes 6291464 | tf_op jit(solution)/shard_map/ppermute | solution.py:350
  44.7 65.0 %collective-permute-start.8 = (bf16[64,32,512]{2,1,0:T(8,128)(2,1)}, bf16[64,32,512]{2,1,0:T(8,128)(2,1)}, u32[]{:S(2)}, u32[]{:S(2)}) collective-permute-start(bf16[64,32,512]{2,1,0:T(8,128)(2,1)} %get-tuple-element.30.refs_1_), channel_id=1, source_target_pairs={{0,6},{1,7},{2,0},{3,1},{4,2},{5,3},{6,4},{7,5},{8,14},{9,15},{10,... | collective-permute-start | bytes 6291464 | tf_op jit(solution)/shard_map/ppermute | solution.py:350
  64.8 47.5 %collective-permute-start.2 = (bf16[64,32,512]{2,1,0:T(8,128)(2,1)}, bf16[64,32,512]{2,1,0:T(8,128)(2,1)S(1)}, u32[]{:S(2)}, u32[]{:S(2)}) collective-permute-start(bf16[64,32,512]{2,1,0:T(8,128)(2,1)} %collective-permute-done.refs_2_), channel_id=1, source_target_pairs={{0,2},{1,3},{2,4},{3,5},{4,6},{5,7},{6,0},{7,1},{8,10},{9,11},{10,... | collective-permute-start | bytes 6291464 | tf_op jit(solution)/shard_map/ppermute | solution.py:350
  65.0 91.6 %collective-permute-start.7 = (bf16[64,32,512]{2,1,0:T(8,128)(2,1)}, bf16[64,32,512]{2,1,0:T(8,128)(2,1)}, u32[]{:S(2)}, u32[]{:S(2)}) collective-permute-start(bf16[64,32,512]{2,1,0:T(8,128)(2,1)} %get-tuple-element.30.refs_1_), channel_id=1, source_target_pairs={{0,2},{1,3},{2,4},{3,5},{4,6},{5,7},{6,0},{7,1},{8,10},{9,11},{10,... | collective-permute-start | bytes 6291464 | tf_op jit(solution)/shard_map/ppermute | solution.py:350
  66.4 92.9 %collective-permute-start.4 = (bf16[64,32,512]{2,1,0:T(8,128)(2,1)}, bf16[64,32,512]{2,1,0:T(8,128)(2,1)}, u32[]{:S(2)}, u32[]{:S(2)}) collective-permute-start(bf16[64,32,512]{2,1,0:T(8,128)(2,1)} %collective-permute-done.refs_2_), channel_id=1, source_target_pairs={{0,1},{1,0},{2,3},{3,2},{4,5},{5,4},{6,7},{7,6},{8,9},{9,8},{10,11... | collective-permute-start | bytes 6291464 | tf_op jit(solution)/shard_map/ppermute | solution.py:350
  68.4 90.9 %collective-permute-start.5 = (bf16[64,32,512]{2,1,0:T(8,128)(2,1)}, bf16[64,32,512]{2,1,0:T(8,128)(2,1)}, u32[]{:S(2)}, u32[]{:S(2)}) collective-permute-start(bf16[64,32,512]{2,1,0:T(8,128)(2,1)} %collective-permute-done.1.refs_3_), channel_id=1, source_target_pairs={{0,1},{1,0},{2,3},{3,2},{4,5},{5,4},{6,7},{7,6},{8,9},{9,8},{10,11... | collective-permute-start | bytes 6291464 | tf_op jit(solution)/shard_map/ppermute | solution.py:350
  109.7 50.1 %collective-permute-start.9 = (bf16[64,32,512]{2,1,0:T(8,128)(2,1)}, bf16[64,32,512]{2,1,0:T(8,128)(2,1)}, u32[]{:S(2)}, u32[]{:S(2)}) collective-permute-start(bf16[64,32,512]{2,1,0:T(8,128)(2,1)} %collective-permute-done.8.refs_3_), channel_id=1, source_target_pairs={{0,6},{1,7},{2,0},{3,1},{4,2},{5,3},{6,4},{7,5},{8,14},{9,15},{10,... | collective-permute-start | bytes 6291464 | tf_op jit(solution)/shard_map/ppermute | solution.py:350
  112.3 48.9 %collective-permute-start.6 = (bf16[64,32,512]{2,1,0:T(8,128)(2,1)S(1)}, bf16[64,32,512]{2,1,0:T(8,128)(2,1)}, u32[]{:S(2)}, u32[]{:S(2)}) collective-permute-start(bf16[64,32,512]{2,1,0:T(8,128)(2,1)S(1)} %collective-permute-done.2.refs_4_), channel_id=1, source_target_pairs={{0,1},{1,0},{2,3},{3,2},{4,5},{5,4},{6,7},{7,6},{8,9},{9,8},{10,11... | collective-permute-start | bytes 6291464 | tf_op jit(solution)/shard_map/ppermute | solution.py:350
  156.7 37.3 %collective-permute-start.10 = (bf16[64,32,512]{2,1,0:T(8,128)(2,1)}, bf16[64,32,512]{2,1,0:T(8,128)(2,1)}, u32[]{:S(2)}, u32[]{:S(2)}) collective-permute-start(bf16[64,32,512]{2,1,0:T(8,128)(2,1)} %get-tuple-element.30.refs_1_), channel_id=1, source_target_pairs={{0,1},{1,0},{2,3},{3,2},{4,5},{5,4},{6,7},{7,6},{8,9},{9,8},{10,11... | collective-permute-start | bytes 6291464 | tf_op jit(solution)/shard_map/ppermute | solution.py:350
  159.3 34.7 %collective-permute-start.12 = (bf16[64,32,512]{2,1,0:T(8,128)(2,1)}, bf16[64,32,512]{2,1,0:T(8,128)(2,1)}, u32[]{:S(2)}, u32[]{:S(2)}) collective-permute-start(bf16[64,32,512]{2,1,0:T(8,128)(2,1)} %collective-permute-done.8.refs_3_), channel_id=1, source_target_pairs={{0,1},{1,0},{2,3},{3,2},{4,5},{5,4},{6,7},{7,6},{8,9},{9,8},{10,11... | collective-permute-start | bytes 6291464 | tf_op jit(solution)/shard_map/ppermute | solution.py:350
  159.3 34.6 %collective-permute-start.11 = (bf16[64,32,512]{2,1,0:T(8,128)(2,1)}, bf16[64,32,512]{2,1,0:T(8,128)(2,1)}, u32[]{:S(2)}, u32[]{:S(2)}) collective-permute-start(bf16[64,32,512]{2,1,0:T(8,128)(2,1)} %collective-permute-done.7.refs_2_), channel_id=1, source_target_pairs={{0,1},{1,0},{2,3},{3,2},{4,5},{5,4},{6,7},{7,6},{8,9},{9,8},{10,11... | collective-permute-start | bytes 6291464 | tf_op jit(solution)/shard_map/ppermute | solution.py:350
  159.8 34.1 %collective-permute-start.13 = (bf16[64,32,512]{2,1,0:T(8,128)(2,1)}, bf16[64,32,512]{2,1,0:T(8,128)(2,1)}, u32[]{:S(2)}, u32[]{:S(2)}) collective-permute-start(bf16[64,32,512]{2,1,0:T(8,128)(2,1)} %collective-permute-done.9.refs_4_), channel_id=1, source_target_pairs={{0,1},{1,0},{2,3},{3,2},{4,5},{5,4},{6,7},{7,6},{8,9},{9,8},{10,11... | collective-permute-start | bytes 6291464 | tf_op jit(solution)/shard_map/ppermute | solution.py:350
  193.8 73.2 %collective-permute-start.14 = (bf16[64,64,256]{2,1,0:T(8,128)(2,1)}, bf16[64,64,256]{2,1,0:T(8,128)(2,1)}, u32[]{:S(2)}, u32[]{:S(2)}) collective-permute-start(bf16[64,64,256]{2,1,0:T(8,128)(2,1)} %get-tuple-element.32.refs_2_), channel_id=1, source_target_pairs={{0,2},{1,3},{2,4},{3,5},{4,6},{5,7},{6,0},{7,1},{8,10},{9,11},{10,... | collective-permute-start | bytes 6291464 | tf_op jit(solution)/shard_map/ppermute | solution.py:350
  227.2 37.4 %collective-permute-start.21 = (bf16[64,32,256]{2,1,0:T(8,128)(2,1)}, bf16[64,32,256]{2,1,0:T(8,128)(2,1)S(1)}, u32[]{:S(2)}, u32[]{:S(2)}) collective-permute-start(bf16[64,32,256]{2,1,0:T(8,128)(2,1)} %get-tuple-element.33.refs_10_), channel_id=1, source_target_pairs={{0,2},{1,3},{2,4},{3,5},{4,6},{5,7},{6,0},{7,1},{8,10},{9,11},{10,... | collective-permute-start | bytes 3145736 | tf_op jit(solution)/shard_map/ppermute | solution.py:350
  227.6 39.1 %collective-permute-start.22 = (bf16[64,32,256]{2,1,0:T(8,128)(2,1)}, bf16[64,32,256]{2,1,0:T(8,128)(2,1)}, u32[]{:S(2)}, u32[]{:S(2)}) collective-permute-start(bf16[64,32,256]{2,1,0:T(8,128)(2,1)} %get-tuple-element.33.refs_10_), channel_id=1, source_target_pairs={{0,6},{1,7},{2,0},{3,1},{4,2},{5,3},{6,4},{7,5},{8,14},{9,15},{10,... | collective-permute-start | bytes 3145736 | tf_op jit(solution)/shard_map/ppermute | solution.py:350
  229.9 57.1 %collective-permute-start.31 = (bf16[64,32,256]{2,1,0:T(8,128)(2,1)}, bf16[64,32,256]{2,1,0:T(8,128)(2,1)S(1)}, u32[]{:S(2)}, u32[]{:S(2)}) collective-permute-start(bf16[64,32,256]{2,1,0:T(8,128)(2,1)} %get-tuple-element.36.refs_10_), channel_id=1, source_target_pairs={{0,2},{1,3},{2,4},{3,5},{4,6},{5,7},{6,0},{7,1},{8,10},{9,11},{10,... | collective-permute-start | bytes 3145736 | tf_op jit(solution)/shard_map/ppermute | solution.py:350
  229.9 58.3 %collective-permute-start.32 = (bf16[64,32,256]{2,1,0:T(8,128)(2,1)}, bf16[64,32,256]{2,1,0:T(8,128)(2,1)S(1)}, u32[]{:S(2)}, u32[]{:S(2)}) collective-permute-start(bf16[64,32,256]{2,1,0:T(8,128)(2,1)} %get-tuple-element.36.refs_10_), channel_id=1, source_target_pairs={{0,6},{1,7},{2,0},{3,1},{4,2},{5,3},{6,4},{7,5},{8,14},{9,15},{10,... | collective-permute-start | bytes 3145736 | tf_op jit(solution)/shard_map/ppermute | solution.py:350
  266.7 100.0 %collective-permute-start.15 = (bf16[64,64,256]{2,1,0:T(8,128)(2,1)S(1)}, bf16[64,64,256]{2,1,0:T(8,128)(2,1)S(1)}, u32[]{:S(2)}, u32[]{:S(2)}) collective-permute-start(bf16[64,64,256]{2,1,0:T(8,128)(2,1)S(1)} %copy-done), channel_id=1, source_target_pairs={{0,6},{1,7},{2,0},{3,1},{4,2},{5,3},{6,4},{7,5},{8,14},{9,15},{10,... | collective-permute-start | bytes 6291464 | tf_op jit(solution)/shard_map/ppermute | solution.py:350
  267.1 100.1 %collective-permute-start.16 = (bf16[64,64,256]{2,1,0:T(8,128)(2,1)}, bf16[64,64,256]{2,1,0:T(8,128)(2,1)S(1)}, u32[]{:S(2)}, u32[]{:S(2)}) collective-permute-start(bf16[64,64,256]{2,1,0:T(8,128)(2,1)} %collective-permute-done.14.refs_3_), channel_id=1, source_target_pairs={{0,2},{1,3},{2,4},{3,5},{4,6},{5,7},{6,0},{7,1},{8,10},{9,11},{10,... | collective-permute-start | bytes 6291464 | tf_op jit(solution)/shard_map/ppermute | solution.py:350
  287.1 56.1 %collective-permute-start.23 = (bf16[64,32,256]{2,1,0:T(8,128)(2,1)}, bf16[64,32,256]{2,1,0:T(8,128)(2,1)}, u32[]{:S(2)}, u32[]{:S(2)}) collective-permute-start(bf16[64,32,256]{2,1,0:T(8,128)(2,1)} %collective-permute-done.22.refs_12_), channel_id=1, source_target_pairs={{0,6},{1,7},{2,0},{3,1},{4,2},{5,3},{6,4},{7,5},{8,14},{9,15},{10,... | collective-permute-start | bytes 3145736 | tf_op jit(solution)/shard_map/ppermute | solution.py:350
  288.2 77.3 %collective-permute-start.33 = (bf16[64,32,256]{2,1,0:T(8,128)(2,1)S(1)}, bf16[64,32,256]{2,1,0:T(8,128)(2,1)S(1)}, u32[]{:S(2)}, u32[]{:S(2)}) collective-permute-start(bf16[64,32,256]{2,1,0:T(8,128)(2,1)S(1)} %collective-permute-done.32.refs_12_), channel_id=1, source_target_pairs={{0,6},{1,7},{2,0},{3,1},{4,2},{5,3},{6,4},{7,5},{8,14},{9,15},{10,... | collective-permute-start | bytes 3145736 | tf_op jit(solution)/shard_map/ppermute | solution.py:350
  288.6 78.1 %collective-permute-start.35 = (bf16[64,32,256]{2,1,0:T(8,128)(2,1)S(1)}, bf16[64,32,256]{2,1,0:T(8,128)(2,1)}, u32[]{:S(2)}, u32[]{:S(2)}) collective-permute-start(bf16[64,32,256]{2,1,0:T(8,128)(2,1)S(1)} %collective-permute-done.31.refs_11_), channel_id=1, source_target_pairs={{0,1},{1,0},{2,3},{3,2},{4,5},{5,4},{6,7},{7,6},{8,9},{9,8},{10,11... | collective-permute-start | bytes 3145736 | tf_op jit(solution)/shard_map/ppermute | solution.py:350
  369.3 44.2 %collective-permute-start.24 = (bf16[64,32,256]{2,1,0:T(8,128)(2,1)}, bf16[64,32,256]{2,1,0:T(8,128)(2,1)}, u32[]{:S(2)}, u32[]{:S(2)}) collective-permute-start(bf16[64,32,256]{2,1,0:T(8,128)(2,1)} %get-tuple-element.33.refs_10_), channel_id=1, source_target_pairs={{0,1},{1,0},{2,3},{3,2},{4,5},{5,4},{6,7},{7,6},{8,9},{9,8},{10,11... | collective-permute-start | bytes 3145736 | tf_op jit(solution)/shard_map/ppermute | solution.py:350
  379.4 34.1 %collective-permute-start.26 = (bf16[64,32,256]{2,1,0:T(8,128)(2,1)}, bf16[64,32,256]{2,1,0:T(8,128)(2,1)}, u32[]{:S(2)}, u32[]{:S(2)}) collective-permute-start(bf16[64,32,256]{2,1,0:T(8,128)(2,1)} %collective-permute-done.22.refs_12_), channel_id=1, source_target_pairs={{0,1},{1,0},{2,3},{3,2},{4,5},{5,4},{6,7},{7,6},{8,9},{9,8},{10,11... | collective-permute-start | bytes 3145736 | tf_op jit(solution)/shard_map/ppermute | solution.py:350
  379.8 33.7 %collective-permute-start.25 = (bf16[64,32,256]{2,1,0:T(8,128)(2,1)S(1)}, bf16[64,32,256]{2,1,0:T(8,128)(2,1)}, u32[]{:S(2)}, u32[]{:S(2)}) collective-permute-start(bf16[64,32,256]{2,1,0:T(8,128)(2,1)S(1)} %collective-permute-done.21.refs_11_), channel_id=1, source_target_pairs={{0,1},{1,0},{2,3},{3,2},{4,5},{5,4},{6,7},{7,6},{8,9},{9,8},{10,11... | collective-permute-start | bytes 3145736 | tf_op jit(solution)/shard_map/ppermute | solution.py:350
  379.9 33.6 %collective-permute-start.27 = (bf16[64,32,256]{2,1,0:T(8,128)(2,1)}, bf16[64,32,256]{2,1,0:T(8,128)(2,1)}, u32[]{:S(2)}, u32[]{:S(2)}) collective-permute-start(bf16[64,32,256]{2,1,0:T(8,128)(2,1)} %collective-permute-done.23.refs_13_), channel_id=1, source_target_pairs={{0,1},{1,0},{2,3},{3,2},{4,5},{5,4},{6,7},{7,6},{8,9},{9,8},{10,11... | collective-permute-start | bytes 3145736 | tf_op jit(solution)/shard_map/ppermute | solution.py:350
  407.3 32.0 %all-to-all-start.1 = ((bf16[4,16,64,256]{3,2,1,0:T(8,128)(2,1)}), bf16[4,16,64,256]{3,2,1,0:T(8,128)(2,1)S(1)}, u32[]{:S(2)}, u32[]{:S(2)}) async-start(bf16[4,16,64,256]{3,2,1,0:T(8,128)(2,1)} %bitcast.109), calls=%async_computation.1 | async-start | bytes 4194304 | tf_op jit(solution)/shard_map/all_to_all | solution.py:423
  440.6 29.5 %all-to-all-start = ((bf16[4,16,64,256]{3,2,1,0:T(8,128)(2,1)}), bf16[4,16,64,256]{3,2,1,0:T(8,128)(2,1)}, u32[]{:S(2)}, u32[]{:S(2)}) async-start(bf16[4,16,64,256]{3,2,1,0:T(8,128)(2,1)} %bitcast.110), calls=%async_computation | async-start | bytes 4194304 | tf_op jit(solution)/shard_map/all_to_all | solution.py:423
  452.7 28.3 %collective-permute-start.38 = (bf16[16,64,256]{2,1,0:T(8,128)(2,1)}, bf16[16,64,256]{2,1,0:T(8,128)(2,1)S(1)}, u32[]{:S(2)}, u32[]{:S(2)}) collective-permute-start(bf16[16,64,256]{2,1,0:T(8,128)(2,1)} %shard_map.233.refs_0_), channel_id=1, source_target_pairs={{0,8},{8,16},{16,24},{24,0},{1,9},{9,17},{17,25},{25,1},{2,10},{10... | collective-permute-start | bytes 1572872 | tf_op jit(solution)/shard_map/ppermute | solution.py:350
  481.0 26.8 %collective-permute-start.28 = (bf16[16,64,256]{2,1,0:T(8,128)(2,1)}, bf16[16,64,256]{2,1,0:T(8,128)(2,1)S(1)}, u32[]{:S(2)}, u32[]{:S(2)}) collective-permute-start(bf16[16,64,256]{2,1,0:T(8,128)(2,1)} %shard_map.231.refs_0_), channel_id=1, source_target_pairs={{0,8},{8,16},{16,24},{24,0},{1,9},{9,17},{17,25},{25,1},{2,10},{10... | collective-permute-start | bytes 1572872 | tf_op jit(solution)/shard_map/ppermute | solution.py:350
  (52 other events, 1036.4 us)
